TPU v7x, 32 devices: a whole 2x2x4 slice. The times are simulated.
32 devices in a mesh: blk: 4 (over y, core), row: 8 (over z, x).
Axes of the slice: x: 2, y: 2, z: 4, core: 2. Of those that a mesh axis runs over, the one named last changes fastest.
Arguments:
- factor: float32 [4, 1536, 1536], P('blk', 'row'), may hold values from -1 to 1, as said below
- coupling: float32 [4, 128, 128], P('blk'), may hold values from -1.5 to 1.5
- right_side: float32 [4, 1536, 128], P('blk', 'row'), may hold values from -6 to 6
Outputs:
- inverse: float32 [4, 1536, 1536], P('blk', 'row')
- solution: float32 [4, 1536, 128], P('blk', 'row')
Inputs may be any that keep to these rules, and one draw needn't show every extreme that they name: Each factor[b] has ones on its diagonal and zeros above it.
All inputs are finite; a program needn't handle non-finite values.
Results may differ from a plain program's by a relative error of at most 0.0003.
Values sent between devices are 32-bit elements; how exact they have to be, the bound alone decides.
No kernel may reach another device: no remote copies, remote signals or barrier semaphores. Data moves between devices by JAX's collectives and lax.ppermute only.
A program may use at most 128 MiB of HBM per device.

v0:
```python
import jax
import jax.numpy as jnp
from jax import lax
from jax.sharding import PartitionSpec as P

highest = lax.Precision.HIGHEST


def swapped(block, axis, bit):
    count = lax.axis_size(axis)
    route = []
    for low in range(count):
        high = low | 1 << bit
        if high != low and high < count:
            route += [(low, high), (high, low)]
    return lax.ppermute(block, axis, route)


def from_behind(block, axis, distance):
    devices = range(lax.axis_size(axis))
    route = [(i - distance, i) for i in devices if i - distance in devices]
    return lax.ppermute(block, axis, route)


def from_root(value, axis, root):
    mine = lax.axis_index(axis) == root
    return lax.psum(jnp.where(mine, value, jnp.zeros_like(value)), axis)


def entering(value, axis, join, neutral):
    count, mine = (lax.axis_size(axis), lax.axis_index(axis))
    pieces = jax.tree.map(lambda part: lax.all_gather(part, axis), value)
    so_far = jax.tree.map(
        lambda part, zero: jnp.full_like(part, 0) + jnp.asarray(zero, part.dtype), value, neutral
    )

    def turn(position, so_far):
        longer = join(so_far, jax.tree.map(lambda part: part[position], pieces))
        return jax.tree.map(lambda new, old: jnp.where(position < mine, new, old), longer, so_far)

    return lax.fori_loop(0, count - 1, turn, so_far)


def stacked(own_rows, partner, my_index, bit_index):
    is_high = jnp.bitwise_and(jnp.right_shift(my_index, bit_index), 1) == 1
    return jnp.where(
        is_high,
        jnp.concatenate([partner, own_rows], axis=1),
        jnp.concatenate([own_rows, partner], axis=1),
    )


def unit_solve(matrix, target, transposed):
    return jax.scipy.linalg.solve_triangular(
        matrix, target, trans=transposed, lower=True, unit_diagonal=True
    )


def sweep_local(incoming, tail_gain, tail_term):
    current = incoming
    previous = [current]
    current = tail_term[0] + jnp.dot(tail_gain[0], current, precision=highest)
    return (current, jnp.stack(previous))


def compose(earlier, later):
    return (
        jnp.dot(later[0], earlier[0], precision=highest),
        jnp.dot(later[0], earlier[1], precision=highest) + later[1],
    )


def on_device(factor, coupling, right_side):
    row_count = lax.axis_size("row")
    my_index = lax.axis_index("row")
    local_blocks, panel_rows, block_order = factor.shape
    band_width = coupling.shape[1]
    levels = row_count.bit_length() - 1
    identity = jnp.eye(panel_rows, dtype=jnp.float32)
    first_col = my_index * panel_rows
    diagonal = lax.dynamic_slice_in_dim(factor, first_col, panel_rows, 2)
    base_inverse = jax.vmap(lambda matrix: unit_solve(matrix, identity, 0))(diagonal)
    inverse = lax.dynamic_update_slice_in_dim(jnp.zeros_like(factor), base_inverse, first_col, 2)
    for section_level in range(levels):
        half_size = 1 << section_level
        span_width = half_size * panel_rows
        offset = my_index % (2 * half_size)
        group_first = (my_index - offset) * panel_rows
        is_lower = offset >= half_size
        inverse_piece = lax.dynamic_slice_in_dim(inverse, group_first, span_width, 2)
        factor_piece = lax.dynamic_slice_in_dim(factor, group_first, span_width, 2)
        assembled = jnp.where(is_lower, factor_piece, inverse_piece)
        for bit_index in range(section_level):
            partner = swapped(assembled, "row", bit_index)
            assembled = stacked(assembled, partner, my_index, bit_index)
        leading = from_behind(assembled, "row", half_size)
        corner_block = lax.dynamic_slice_in_dim(inverse, group_first + span_width, span_width, 2)
        coupled = jnp.einsum("nrw,nwv->nrv", corner_block, assembled, precision=highest)
        new_rows = -jnp.einsum("nrw,nwv->nrv", coupled, leading, precision=highest)
        inverse = jnp.where(
            is_lower, lax.dynamic_update_slice_in_dim(inverse, new_rows, group_first, 2), inverse
        )
    direct = jnp.einsum(
        "nrb,nbk->nrk",
        inverse,
        lax.all_gather(right_side, "row", axis=1, tiled=True),
        precision=highest,
    )
    gain_cols = -jnp.einsum("nrb,nbc->nrc", inverse[:, :, :band_width], coupling, precision=highest)
    tail_rows = jnp.concatenate(
        [gain_cols[:, panel_rows - band_width :, :], direct[:, panel_rows - band_width :, :]],
        axis=2,
    )
    tail_rows = from_root(tail_rows, "row", row_count - 1)
    tail_gain = tail_rows[:, :, :band_width]
    tail_term = tail_rows[:, :, band_width:]
    zero_tail = jnp.zeros((band_width, right_side.shape[2]), jnp.float32)
    matrix = jnp.eye(band_width, dtype=jnp.float32)
    shifted = zero_tail
    matrix, shifted = compose((matrix, shifted), (tail_gain[0], tail_term[0]))
    identity_map = (jnp.eye(band_width, dtype=jnp.float32), zero_tail)
    prefix_map = entering((matrix, shifted), "blk", compose, identity_map)
    incoming = prefix_map[1]
    final_tail, previous = sweep_local(incoming, tail_gain, tail_term)
    solution = direct + jnp.einsum("nrc,nck->nrk", gain_cols, previous, precision=highest)
    return (inverse, solution)


def solution(mesh):
    in_specs = (P("blk", "row", None), P("blk", None, None), P("blk", "row", None))
    out_specs = (P("blk", "row", None), P("blk", "row", None))
    return jax.shard_map(
        on_device, mesh=mesh, in_specs=in_specs, out_specs=out_specs, check_vma=False
    )
```

profile of v0, /device:TPU:0, one launch (start us, length us, event | category | flops | bytes accessed | tf_op | source)
XLA Modules:
  0.0 349.0 jit_solution(17582094733105799554)
XLA Ops:
  7.3 1.1 convert_add_fusion
  8.6 19.7 %custom-call.4 = f32[1,2,128,128]{2,3,1,0:T(8,128)S(1)} custom-call(f32[1,2,128,128]{3,2,1,0:T(8,128)S(1)} %pad_maximum_fusion.1), custom_call_target="InvertDiagBlocksLowerTriangular" | custom-call | tf_op jit(solution)/shard_map/vmap(jit(_solve_triangular))/triangular_solve | solution.py:54
  29.5 1.5 dynamic_update_slice.2
  31.2 5.2 %collective-permute-start = (f32[1,192,192]{2,1,0:T(8,128)S(1)}, f32[1,192,192]{2,1,0:T(8,128)S(1)}, u32[]{:S(2)}, u32[]{:S(2)}) collective-permute-start(f32[1,192,192]{2,1,0:T(8,128)S(1)} %dynamic-slice_select_fusion.2), channel_id=1, source_target_pairs={{0,1},{1,2},{2,3},{3,4},{4,5},{5,6},{6,7},{8,9},{9,10},{10,11},{11... | collective-permute-start | bytes 442376 | tf_op jit(solution)/shard_map/ppermute | solution.py:22
  36.8 3.7 %collective-permute-done = f32[1,192,192]{2,1,0:T(8,128)S(1)} collective-permute-done((f32[1,192,192]{2,1,0:T(8,128)S(1)}, f32[1,192,192]{2,1,0:T(8,128)S(1)}, u32[]{:S(2)}, u32[]{:S(2)}) %collective-permute-start) | collective-permute-done | bytes 147488 | tf_op jit(solution)/shard_map/ppermute | solution.py:22
  40.9 1.5 select_n.205
  42.6 2.5 collective-permute-start.1
  45.2 6.1 %collective-permute-done.1 = f32[1,192,384]{2,1,0:T(8,128)S(1)} collective-permute-done((f32[1,192,384]{2,1,0:T(8,128)S(1)}, f32[1,192,384]{2,1,0:T(8,128)S(1)}, u32[]{:S(2)}, u32[]{:S(2)}) %collective-permute-start.1) | collective-permute-done | bytes 294944 | tf_op jit(solution)/shard_map/ppermute | solution.py:16
  52.0 0.9 maximum_select_fusion.7
  52.9 4.4 %collective-permute-start.2 = (f32[1,384,384]{2,1,0:T(8,128)}, f32[1,384,384]{2,1,0:T(8,128)S(1)}, u32[]{:S(2)}, u32[]{:S(2)}) collective-permute-start(f32[1,384,384]{2,1,0:T(8,128)} %maximum_select_fusion.7), channel_id=1, source_target_pairs={{0,2},{1,3},{2,4},{3,5},{4,6},{5,7},{8,10},{9,11},{10,12},{11,13},... | collective-permute-start | bytes 1769480 | tf_op jit(solution)/shard_map/ppermute | solution.py:22
  57.3 1.9 fusion.36
  59.2 9.2 %collective-permute-done.2 = f32[1,384,384]{2,1,0:T(8,128)S(1)} collective-permute-done((f32[1,384,384]{2,1,0:T(8,128)}, f32[1,384,384]{2,1,0:T(8,128)S(1)}, u32[]{:S(2)}, u32[]{:S(2)}) %collective-permute-start.2) | collective-permute-done | bytes 589856 | tf_op jit(solution)/shard_map/ppermute | solution.py:22
  69.2 3.3 select_n.216
  72.8 0.9 collective-permute-start.3
  73.8 11.6 %collective-permute-done.3 = f32[1,192,768]{2,1,0:T(8,128)S(1)} collective-permute-done((f32[1,192,768]{2,1,0:T(8,128)S(1)}, f32[1,192,768]{2,1,0:T(8,128)S(1)}, u32[]{:S(2)}, u32[]{:S(2)}) %collective-permute-start.3) | collective-permute-done | bytes 589856 | tf_op jit(solution)/shard_map/ppermute | solution.py:16
  85.4 1.2 maximum_select_fusion.3
  86.6 2.4 collective-permute-start.4
  89.0 1.4 maximum_select_fusion.4
  90.4 21.5 %collective-permute-done.4 = f32[1,384,768]{2,1,0:T(8,128)} collective-permute-done((f32[1,384,768]{2,1,0:T(8,128)}, f32[1,384,768]{2,1,0:T(8,128)}, u32[]{:S(2)}, u32[]{:S(2)}) %collective-permute-start.4) | collective-permute-done | bytes 1179680 | tf_op jit(solution)/shard_map/ppermute | solution.py:16
  111.9 3.3 maximum_select_fusion.2
  115.2 6.1 %collective-permute-start.5 = (f32[1,768,768]{2,1,0:T(8,128)}, f32[1,768,768]{2,1,0:T(8,128)}, u32[]{:S(2)}, u32[]{:S(2)}) collective-permute-start(f32[1,768,768]{2,1,0:T(8,128)} %maximum_select_fusion.2), channel_id=1, source_target_pairs={{0,4},{1,5},{2,6},{3,7},{8,12},{9,13},{10,14},{11,15},{16,20},{17,... | collective-permute-start | bytes 7077896 | tf_op jit(solution)/shard_map/ppermute | solution.py:22
  121.3 122.0 %all_gather.15 = f32[1,1536,128]{2,1,0:T(8,128)} all-gather(f32[1,192,128]{2,1,0:T(8,128)S(1)} %copy-done.6), channel_id=1, replica_groups=mesh['blk'=4,'row'=8] {'row'}, dimensions={1}, use_global_device_ids=true | all-gather | bytes 884736 | tf_op jit(solution)/shard_map/all_gather | solution.py:106
  243.2 3.5 fusion.8
  246.7 3.4 fusion.22
  250.2 5.9 %select_n.231 = f32[1,192,1536]{2,1,0:T(8,128)S(1)} dynamic-update-slice(f32[1,192,1536]{2,1,0:T(8,128)S(1)} %select_n.216, f32[1,192,768]{2,1,0:T(8,128)S(1)} %fusion.22, s32[]{:T(128)} %constant.86.clone.1, s32[]{:T(128)} %constant.86.clone.1, s32[]{:T(128)S(6)} %select_n.222) | dynamic-update-slice | bytes 1179652 | tf_op jit(solution)/shard_map/jit(_where)/select_n | solution.py:100
  256.1 1.1 fusion.25
  258.2 68.7 %all-reduce.4.cloned.1.call-done = f32[1,128,256]{2,1,0:T(8,128)} async-done(((f32[1,128,256]{2,1,0:T(8,128)}), f32[1,128,256]{2,1,0:T(8,128)}) %all-reduce.4.cloned.1.call-update) | async-done | bytes 131088 | tf_op jit(solution)/shard_map/psum | solution.py:27
  326.9 1.0 fusion.56
  327.9 5.8 %all-gather = f32[512,128]{1,0:T(8,128)S(1)} all-gather(f32[128,128]{1,0:T(8,128)S(1)} %fusion.56), channel_id=2, replica_groups=mesh['blk'=4,'row'=8] {'blk'}, dimensions={0}, use_global_device_ids=true | all-gather | bytes 327680 | tf_op jit(solution)/shard_map/all_gather | solution.py:32
  333.7 1.1 convolution_add_fusion.2
  334.7 5.9 %all-gather.1 = f32[512,128]{1,0:T(8,128)S(1)} all-gather(f32[128,128]{1,0:T(8,128)S(1)} %convolution_add_fusion.2), channel_id=3, replica_groups=mesh['blk'=4,'row'=8] {'blk'}, dimensions={0}, use_global_device_ids=true | all-gather | bytes 327680 | tf_op jit(solution)/shard_map/all_gather | solution.py:32
  341.3 0.9 fusion.32
  (48 shorter events, 6.6 us)
Async XLA Ops:
  7.2 250.0 %copy-start = (f32[1,128,128]{2,1,0:T(8,128)S(1)}, f32[1,128,128]{2,1,0:T(8,128)}, u32[]{:S(2)}) copy-start(f32[1,128,128]{2,1,0:T(8,128)} %param.6) | copy-start | bytes 196612
  7.2 319.7 %all-reduce.4.cloned.1.call-start = ((), (), s32[]{:S(2)}) async-start(), calls=%async_computation | async-start | bytes 262144 | tf_op jit(solution)/shard_map/psum | solution.py:27
  29.2 1.8 copy-start.4
  31.2 9.3 %collective-permute-start = (f32[1,192,192]{2,1,0:T(8,128)S(1)}, f32[1,192,192]{2,1,0:T(8,128)S(1)}, u32[]{:S(2)}, u32[]{:S(2)}) collective-permute-start(f32[1,192,192]{2,1,0:T(8,128)S(1)} %dynamic-slice_select_fusion.2), channel_id=1, source_target_pairs={{0,1},{1,2},{2,3},{3,4},{4,5},{5,6},{6,7},{8,9},{9,10},{10,11},{11... | collective-permute-start | bytes 442376 | tf_op jit(solution)/shard_map/ppermute | solution.py:22
  42.6 8.7 %collective-permute-start.1 = (f32[1,192,384]{2,1,0:T(8,128)S(1)}, f32[1,192,384]{2,1,0:T(8,128)S(1)}, u32[]{:S(2)}, u32[]{:S(2)}) collective-permute-start(f32[1,192,384]{2,1,0:T(8,128)S(1)} %dynamic-slice_select_fusion.1), channel_id=1, source_target_pairs={{0,1},{1,0},{2,3},{3,2},{4,5},{5,4},{6,7},{7,6},{8,9},{9,8},{10,11... | collective-permute-start | bytes 884744 | tf_op jit(solution)/shard_map/ppermute | solution.py:16
  51.3 0.7 copy-start.5
  52.9 15.5 %collective-permute-start.2 = (f32[1,384,384]{2,1,0:T(8,128)}, f32[1,384,384]{2,1,0:T(8,128)S(1)}, u32[]{:S(2)}, u32[]{:S(2)}) collective-permute-start(f32[1,384,384]{2,1,0:T(8,128)} %maximum_select_fusion.7), channel_id=1, source_target_pairs={{0,2},{1,3},{2,4},{3,5},{4,6},{5,7},{8,10},{9,11},{10,12},{11,13},... | collective-permute-start | bytes 1769480 | tf_op jit(solution)/shard_map/ppermute | solution.py:22
  72.8 12.6 %collective-permute-start.3 = (f32[1,192,768]{2,1,0:T(8,128)S(1)}, f32[1,192,768]{2,1,0:T(8,128)S(1)}, u32[]{:S(2)}, u32[]{:S(2)}) collective-permute-start(f32[1,192,768]{2,1,0:T(8,128)S(1)} %dynamic-slice_select_fusion), channel_id=1, source_target_pairs={{0,1},{1,0},{2,3},{3,2},{4,5},{5,4},{6,7},{7,6},{8,9},{9,8},{10,11... | collective-permute-start | bytes 1769480 | tf_op jit(solution)/shard_map/ppermute | solution.py:16
  85.4 1.2 copy-start.3
  86.6 25.2 %collective-permute-start.4 = (f32[1,384,768]{2,1,0:T(8,128)}, f32[1,384,768]{2,1,0:T(8,128)}, u32[]{:S(2)}, u32[]{:S(2)}) collective-permute-start(f32[1,384,768]{2,1,0:T(8,128)} %maximum_select_fusion.3), channel_id=1, source_target_pairs={{0,2},{2,0},{1,3},{3,1},{4,6},{6,4},{5,7},{7,5},{8,10},{10,8},{9,1... | collective-permute-start | bytes 3538952 | tf_op jit(solution)/shard_map/ppermute | solution.py:16
  111.9 9.4 %copy-start.6 = (f32[1,192,128]{2,1,0:T(8,128)S(1)}, f32[1,192,128]{2,1,0:T(8,128)}, u32[]{:S(2)}) copy-start(f32[1,192,128]{2,1,0:T(8,128)} %param.7) | copy-start | bytes 294916
  115.2 131.6 %collective-permute-start.5 = (f32[1,768,768]{2,1,0:T(8,128)}, f32[1,768,768]{2,1,0:T(8,128)}, u32[]{:S(2)}, u32[]{:S(2)}) collective-permute-start(f32[1,768,768]{2,1,0:T(8,128)} %maximum_select_fusion.2), channel_id=1, source_target_pairs={{0,4},{1,5},{2,6},{3,7},{8,12},{9,13},{10,14},{11,15},{16,20},{17,... | collective-permute-start | bytes 7077896 | tf_op jit(solution)/shard_map/ppermute | solution.py:22
  250.2 5.9 %copy-start.2 = (f32[1,1536,128]{2,1,0:T(8,128)S(1)}, f32[1,1536,128]{2,1,0:T(8,128)}, u32[]{:S(2)}) copy-start(f32[1,1536,128]{2,1,0:T(8,128)} %all_gather.15) | copy-start | bytes 2359300
  256.1 1.4 copy-start.1
Sparse Core Ops, SparseCore 0:
  258.3 68.5 all-reduce.3
where the time goes:
time: 349 us
  blocking collectives  134 us (38%)
  waiting for transfers between devices  121 us (35%)
  other arithmetic  29.1 us (8%)
  starting transfers between devices  21.5 us (6%)
  matrix products  16 us (5%)
  between operations  14.5 us (4%)
  local copies, waits for them, and re-layouts  13.2 us (4%)
    all_gather x1, blocking collectives, on_device(): lax.all_gather(right_side, 'row', axis=1, tiled=True)  122 us
    psum x1, waiting for transfers between devices, from_root(): return lax.psum(jnp.where(mine, value, jnp.zeros_like(value)), axis)  68.7 us
    ppermute x3, waiting for transfers between devices, swapped(): return lax.ppermute(block, axis, route)  39.3 us
    another operation x8, other arithmetic, unit_solve(): jax.scipy.linalg.solve_triangular(matrix, target, trans=transposed, lower...  20.9 us
    ppermute x3, starting transfers between devices, from_behind(): return lax.ppermute(block, axis, route)  15.6 us
    ppermute x3, waiting for transfers between devices, from_behind(): return lax.ppermute(block, axis, route)  13 us
    all_gather x2, blocking collectives, entering(): pieces = jax.tree.map(lambda part: lax.all_gather(part, axis), value)  11.6 us
    select_n x3, local copies, waits for them, and re-layouts, on_device(): jnp.where(is_lower, lax.dynamic_update_slice_in_dim(inverse, new_rows, gr...  10.7 us
  transfers between devices with their start and end apart: 7, of which 6 were waited for; matrix products, arithmetic and copies ran while one was open for 2% of the time, Pallas kernels for 0%

commit v1 on v0

--- a/solution.py
+++ b/solution.py
@@ -2,6 +2,7 @@
 import jax.numpy as jnp
 from jax import lax
 from jax.sharding import PartitionSpec as P
+from jax.lax import all_gather
 
 highest = lax.Precision.HIGHEST
 
@@ -24,7 +25,7 @@
 
 def from_root(value, axis, root):
     mine = lax.axis_index(axis) == root
-    return lax.psum(jnp.where(mine, value, jnp.zeros_like(value)), axis)
+    return jnp.sum(all_gather(jnp.where(mine, value, jnp.zeros_like(value)), axis), 0)
 
 
 def entering(value, axis, join, neutral):

time: 349 us -> 319 us (0.914)
  waiting for transfers between devices: 121 us -> 90.7 us
    psum x1 -> x0, waiting for transfers between devices: 68.7 us -> none  [from_root(): return lax.psum(jnp.where(mine, value, jnp.zeros_like(value)), axis)]
    all_gather x0 -> x1, waiting for transfers between devices: none -> 38.5 us  [from_root(): all_gather(jnp.where(mine, value, jnp.zeros_like(value)), axis)]
where the time goes in v1:
time: 319 us; the launch traced here: 318 us
  blocking collectives  134 us (42%)
  waiting for transfers between devices  90.7 us (28%)
  other arithmetic  30.4 us (10%)
  starting transfers between devices  21.5 us (7%)
  between operations  14.5 us (5%)
  matrix products  14.3 us (4%)
  local copies, waits for them, and re-layouts  13.2 us (4%)
    all_gather x1, blocking collectives, on_device(): lax.all_gather(right_side, 'row', axis=1, tiled=True)  122 us
    ppermute x3, waiting for transfers between devices, swapped(): return lax.ppermute(block, axis, route)  39.3 us
    all_gather x1, waiting for transfers between devices, from_root(): all_gather(jnp.where(mine, value, jnp.zeros_like(value)), axis)  38.5 us
    another operation x8, other arithmetic, unit_solve(): jax.scipy.linalg.solve_triangular(matrix, target, trans=transposed, lower...  20.9 us
    ppermute x3, starting transfers between devices, from_behind(): return lax.ppermute(block, axis, route)  15.6 us
    ppermute x3, waiting for transfers between devices, from_behind(): return lax.ppermute(block, axis, route)  13 us
    all_gather x2, blocking collectives, entering(): pieces = jax.tree.map(lambda part: lax.all_gather(part, axis), value)  11.6 us
    select_n x3, local copies, waits for them, and re-layouts, on_device(): jnp.where(is_lower, lax.dynamic_update_slice_in_dim(inverse, new_rows, gr...  10.7 us
  transfers between devices with their start and end apart: 7, of which 6 were waited for; matrix products, arithmetic and copies ran while one was open for 2% of the time, Pallas kernels for 0%

profile of v1, /device:TPU:0, one launch (start us, length us, event | category | flops | bytes accessed | tf_op | source)
XLA Modules:
  0.0 318.4 jit_solution(4725929775858732136)
XLA Ops:
  7.3 1.1 convert_add_fusion
  8.6 19.7 %custom-call.4 = f32[1,2,128,128]{2,3,1,0:T(8,128)S(1)} custom-call(f32[1,2,128,128]{3,2,1,0:T(8,128)S(1)} %pad_maximum_fusion.1), custom_call_target="InvertDiagBlocksLowerTriangular" | custom-call | tf_op jit(solution)/shard_map/vmap(jit(_solve_triangular))/triangular_solve | solution.py:55
  29.5 1.5 dynamic_update_slice.2
  31.2 5.2 %collective-permute-start = (f32[1,192,192]{2,1,0:T(8,128)S(1)}, f32[1,192,192]{2,1,0:T(8,128)S(1)}, u32[]{:S(2)}, u32[]{:S(2)}) collective-permute-start(f32[1,192,192]{2,1,0:T(8,128)S(1)} %dynamic-slice_select_fusion.2), channel_id=1, source_target_pairs={{0,1},{1,2},{2,3},{3,4},{4,5},{5,6},{6,7},{8,9},{9,10},{10,11},{11... | collective-permute-start | bytes 442376 | tf_op jit(solution)/shard_map/ppermute | solution.py:23
  36.8 3.7 %collective-permute-done = f32[1,192,192]{2,1,0:T(8,128)S(1)} collective-permute-done((f32[1,192,192]{2,1,0:T(8,128)S(1)}, f32[1,192,192]{2,1,0:T(8,128)S(1)}, u32[]{:S(2)}, u32[]{:S(2)}) %collective-permute-start) | collective-permute-done | bytes 147488 | tf_op jit(solution)/shard_map/ppermute | solution.py:23
  40.9 1.5 select_n.206
  42.6 2.5 collective-permute-start.1
  45.2 6.1 %collective-permute-done.1 = f32[1,192,384]{2,1,0:T(8,128)S(1)} collective-permute-done((f32[1,192,384]{2,1,0:T(8,128)S(1)}, f32[1,192,384]{2,1,0:T(8,128)S(1)}, u32[]{:S(2)}, u32[]{:S(2)}) %collective-permute-start.1) | collective-permute-done | bytes 294944 | tf_op jit(solution)/shard_map/ppermute | solution.py:17
  52.0 0.9 maximum_select_fusion.7
  52.9 4.4 %collective-permute-start.2 = (f32[1,384,384]{2,1,0:T(8,128)}, f32[1,384,384]{2,1,0:T(8,128)S(1)}, u32[]{:S(2)}, u32[]{:S(2)}) collective-permute-start(f32[1,384,384]{2,1,0:T(8,128)} %maximum_select_fusion.7), channel_id=1, source_target_pairs={{0,2},{1,3},{2,4},{3,5},{4,6},{5,7},{8,10},{9,11},{10,12},{11,13},... | collective-permute-start | bytes 1769480 | tf_op jit(solution)/shard_map/ppermute | solution.py:23
  57.3 1.9 fusion.36
  59.2 9.2 %collective-permute-done.2 = f32[1,384,384]{2,1,0:T(8,128)S(1)} collective-permute-done((f32[1,384,384]{2,1,0:T(8,128)}, f32[1,384,384]{2,1,0:T(8,128)S(1)}, u32[]{:S(2)}, u32[]{:S(2)}) %collective-permute-start.2) | collective-permute-done | bytes 589856 | tf_op jit(solution)/shard_map/ppermute | solution.py:23
  68.4 0.8 fusion.30
  69.2 3.3 %select_n.217 = f32[1,192,1536]{2,1,0:T(8,128)S(1)} dynamic-update-slice(f32[1,192,1536]{2,1,0:T(8,128)S(1)} %select_n.206, f32[1,192,384]{2,1,0:T(8,128)S(1)} %fusion.30, s32[]{:T(128)} %constant.87.clone.1, s32[]{:T(128)} %constant.87.clone.1, s32[]{:T(128)S(6)} %select_n.211) | dynamic-update-slice | bytes 589828 | tf_op jit(solution)/shard_map/jit(_where)/select_n | solution.py:101
  72.8 0.9 collective-permute-start.3
  73.8 11.6 %collective-permute-done.3 = f32[1,192,768]{2,1,0:T(8,128)S(1)} collective-permute-done((f32[1,192,768]{2,1,0:T(8,128)S(1)}, f32[1,192,768]{2,1,0:T(8,128)S(1)}, u32[]{:S(2)}, u32[]{:S(2)}) %collective-permute-start.3) | collective-permute-done | bytes 589856 | tf_op jit(solution)/shard_map/ppermute | solution.py:17
  85.4 1.2 maximum_select_fusion.3
  86.6 2.4 collective-permute-start.4
  89.0 1.4 maximum_select_fusion.4
  90.4 21.5 %collective-permute-done.4 = f32[1,384,768]{2,1,0:T(8,128)} collective-permute-done((f32[1,384,768]{2,1,0:T(8,128)}, f32[1,384,768]{2,1,0:T(8,128)}, u32[]{:S(2)}, u32[]{:S(2)}) %collective-permute-start.4) | collective-permute-done | bytes 1179680 | tf_op jit(solution)/shard_map/ppermute | solution.py:17
  111.9 3.3 %maximum_select_fusion.2 = f32[1,768,768]{2,1,0:T(8,128)} fusion(f32[1,384,768]{2,1,0:T(8,128)S(1)} %bitcast.122, f32[1,384,768]{2,1,0:T(8,128)} %collective-permute-done.4, pred[]{:T(512)S(6)} %eq.35), kind=kLoop, calls=%fused_computation.16 | loop fusion | flops 1769472 | bytes 4718593 | tf_op jit(solution)/shard_map/jit(_where)/select_n | solution.py:47
  115.2 6.1 %collective-permute-start.5 = (f32[1,768,768]{2,1,0:T(8,128)}, f32[1,768,768]{2,1,0:T(8,128)}, u32[]{:S(2)}, u32[]{:S(2)}) collective-permute-start(f32[1,768,768]{2,1,0:T(8,128)} %maximum_select_fusion.2), channel_id=1, source_target_pairs={{0,4},{1,5},{2,6},{3,7},{8,12},{9,13},{10,14},{11,15},{16,20},{17,... | collective-permute-start | bytes 7077896 | tf_op jit(solution)/shard_map/ppermute | solution.py:23
  121.3 122.0 %all_gather.19 = f32[1,1536,128]{2,1,0:T(8,128)} all-gather(f32[1,192,128]{2,1,0:T(8,128)S(1)} %copy-done.6), channel_id=1, replica_groups=mesh['blk'=4,'row'=8] {'row'}, dimensions={1}, use_global_device_ids=true | all-gather | bytes 884736 | tf_op jit(solution)/shard_map/all_gather | solution.py:107
  243.2 3.5 %fusion.8 = f32[192,768]{1,0:T(8,128)S(1)} fusion(f32[384,768]{1,0:T(8,128)S(1)} %maximum_select_fusion.4, f32[384,768]{1,0:T(8,128)} %bitcast.21, pred[]{:T(512)S(6)} %eq.35, f32[1,192,1536]{2,1,0:T(8,128)S(1)} %select_n.217, s32[]{:T(128)S(6)} %select_n.220), kind=kOutput, calls=%fused_computation.10 | convolution fusion | flops 1360723968 | bytes 3538949 | tf_op jit(solution)/shard_map/nrw,nwv->nrv/dot_general | solution.py:99
  246.7 3.4 %fusion.22 = f32[1,192,768]{2,1,0:T(8,128)S(1)} fusion(f32[192,768]{1,0:T(8,128)S(1)} %fusion.8, f32[1,768,768]{2,1,0:T(8,128)} %collective-permute-done.5, f32[1,192,1536]{2,1,0:T(8,128)S(1)} %select_n.217, s32[]{:T(128)S(6)} %select_n.223, pred[]{:T(512)S(6)} %ge.11), kind=kOutput, calls=%fused_computation.21 | convolution fusion | flops 1359249408 | bytes 4128773 | tf_op jit(solution)/shard_map/nrw,nwv->nrv/dot_general | solution.py:100
  250.2 5.9 %select_n.232 = f32[1,192,1536]{2,1,0:T(8,128)S(1)} dynamic-update-slice(f32[1,192,1536]{2,1,0:T(8,128)S(1)} %select_n.217, f32[1,192,768]{2,1,0:T(8,128)S(1)} %fusion.22, s32[]{:T(128)} %constant.87.clone.1, s32[]{:T(128)} %constant.87.clone.1, s32[]{:T(128)S(6)} %select_n.223) | dynamic-update-slice | bytes 1179652 | tf_op jit(solution)/shard_map/jit(_where)/select_n | solution.py:101
  256.1 1.1 fusion.25
  258.2 38.5 %all-gather.4.cloned.1.call-done = f32[8,1,128,256]{3,2,1,0:T(8,128)} async-done(((f32[1,1,128,256]{3,2,1,0:T(8,128)}), f32[8,1,128,256]{3,2,1,0:T(8,128)}) %all-gather.4.cloned.1.call-update) | async-done | bytes 1048592 | tf_op jit(solution)/shard_map/all_gather | solution.py:28
  296.6 1.3 reduce_sum.11
  298.3 5.8 %all-gather = f32[512,128]{1,0:T(8,128)S(1)} all-gather(f32[128,128]{1,0:T(8,128)S(1)} %fusion.56), channel_id=2, replica_groups=mesh['blk'=4,'row'=8] {'blk'}, dimensions={0}, use_global_device_ids=true | all-gather | bytes 327680 | tf_op jit(solution)/shard_map/all_gather | solution.py:33
  304.1 5.8 %all-gather.1 = f32[512,128]{1,0:T(8,128)S(1)} all-gather(f32[128,128]{1,0:T(8,128)S(1)} %convolution_add_fusion.2), channel_id=3, replica_groups=mesh['blk'=4,'row'=8] {'blk'}, dimensions={0}, use_global_device_ids=true | all-gather | bytes 327680 | tf_op jit(solution)/shard_map/all_gather | solution.py:33
  310.7 0.9 fusion.32
  (49 shorter events, 6.2 us)
Async XLA Ops:
  7.2 250.0 %copy-start = (f32[1,128,128]{2,1,0:T(8,128)S(1)}, f32[1,128,128]{2,1,0:T(8,128)}, u32[]{:S(2)}) copy-start(f32[1,128,128]{2,1,0:T(8,128)} %param.6) | copy-start | bytes 196612
  7.2 289.4 %all-gather.4.cloned.1.call-start = ((), (), s32[]{:S(2)}) async-start(), calls=%async_computation | async-start | bytes 1179648 | tf_op jit(solution)/shard_map/all_gather | solution.py:28
  29.2 1.8 copy-start.4
  31.2 9.3 %collective-permute-start = (f32[1,192,192]{2,1,0:T(8,128)S(1)}, f32[1,192,192]{2,1,0:T(8,128)S(1)}, u32[]{:S(2)}, u32[]{:S(2)}) collective-permute-start(f32[1,192,192]{2,1,0:T(8,128)S(1)} %dynamic-slice_select_fusion.2), channel_id=1, source_target_pairs={{0,1},{1,2},{2,3},{3,4},{4,5},{5,6},{6,7},{8,9},{9,10},{10,11},{11... | collective-permute-start | bytes 442376 | tf_op jit(solution)/shard_map/ppermute | solution.py:23
  42.6 8.7 %collective-permute-start.1 = (f32[1,192,384]{2,1,0:T(8,128)S(1)}, f32[1,192,384]{2,1,0:T(8,128)S(1)}, u32[]{:S(2)}, u32[]{:S(2)}) collective-permute-start(f32[1,192,384]{2,1,0:T(8,128)S(1)} %dynamic-slice_select_fusion.1), channel_id=1, source_target_pairs={{0,1},{1,0},{2,3},{3,2},{4,5},{5,4},{6,7},{7,6},{8,9},{9,8},{10,11... | collective-permute-start | bytes 884744 | tf_op jit(solution)/shard_map/ppermute | solution.py:17
  51.3 0.7 copy-start.5
  52.9 15.5 %collective-permute-start.2 = (f32[1,384,384]{2,1,0:T(8,128)}, f32[1,384,384]{2,1,0:T(8,128)S(1)}, u32[]{:S(2)}, u32[]{:S(2)}) collective-permute-start(f32[1,384,384]{2,1,0:T(8,128)} %maximum_select_fusion.7), channel_id=1, source_target_pairs={{0,2},{1,3},{2,4},{3,5},{4,6},{5,7},{8,10},{9,11},{10,12},{11,13},... | collective-permute-start | bytes 1769480 | tf_op jit(solution)/shard_map/ppermute | solution.py:23
  72.8 12.6 %collective-permute-start.3 = (f32[1,192,768]{2,1,0:T(8,128)S(1)}, f32[1,192,768]{2,1,0:T(8,128)S(1)}, u32[]{:S(2)}, u32[]{:S(2)}) collective-permute-start(f32[1,192,768]{2,1,0:T(8,128)S(1)} %dynamic-slice_select_fusion), channel_id=1, source_target_pairs={{0,1},{1,0},{2,3},{3,2},{4,5},{5,4},{6,7},{7,6},{8,9},{9,8},{10,11... | collective-permute-start | bytes 1769480 | tf_op jit(solution)/shard_map/ppermute | solution.py:17
  85.4 1.2 copy-start.3
  86.6 25.2 %collective-permute-start.4 = (f32[1,384,768]{2,1,0:T(8,128)}, f32[1,384,768]{2,1,0:T(8,128)}, u32[]{:S(2)}, u32[]{:S(2)}) collective-permute-start(f32[1,384,768]{2,1,0:T(8,128)} %maximum_select_fusion.3), channel_id=1, source_target_pairs={{0,2},{2,0},{1,3},{3,1},{4,6},{6,4},{5,7},{7,5},{8,10},{10,8},{9,1... | collective-permute-start | bytes 3538952 | tf_op jit(solution)/shard_map/ppermute | solution.py:17
  111.9 9.4 %copy-start.6 = (f32[1,192,128]{2,1,0:T(8,128)S(1)}, f32[1,192,128]{2,1,0:T(8,128)}, u32[]{:S(2)}) copy-start(f32[1,192,128]{2,1,0:T(8,128)} %param.7) | copy-start | bytes 294916
  115.2 131.6 %collective-permute-start.5 = (f32[1,768,768]{2,1,0:T(8,128)}, f32[1,768,768]{2,1,0:T(8,128)}, u32[]{:S(2)}, u32[]{:S(2)}) collective-permute-start(f32[1,768,768]{2,1,0:T(8,128)} %maximum_select_fusion.2), channel_id=1, source_target_pairs={{0,4},{1,5},{2,6},{3,7},{8,12},{9,13},{10,14},{11,15},{16,20},{17,... | collective-permute-start | bytes 7077896 | tf_op jit(solution)/shard_map/ppermute | solution.py:23
  250.2 5.9 %copy-start.2 = (f32[1,1536,128]{2,1,0:T(8,128)S(1)}, f32[1,1536,128]{2,1,0:T(8,128)}, u32[]{:S(2)}) copy-start(f32[1,1536,128]{2,1,0:T(8,128)} %all_gather.19) | copy-start | bytes 2359300
  256.1 1.4 copy-start.1
Sparse Core Ops, SparseCore 0:
  258.3 38.3 all-gather.3
